TPU v7x, 128 devices: a whole 4x4x4 slice. The times are simulated.
128 devices in a mesh: north: 32 (over z, x, core), deep: 4 (over y).
Axes of the slice: x: 4, y: 4, z: 4, core: 2. Of those that a mesh axis runs over, the one named last changes fastest.
Arguments:
- source: float32 [512, 512, 2048], P(None, 'north', 'deep'), may hold values from -6 to 6
- symbol_x: float32 [512], replicated, may hold values from 0.3 to 3
- symbol_y: float32 [512], replicated, may hold values from 0.3 to 3
- symbol_z: float32 [2048], replicated, may hold values from 0.3 to 3
Outputs:
- coefficients: float32 [256, 256, 1024], P('north', 'deep')
All inputs are finite; a program needn't handle non-finite values.
Results may differ from a plain program's by a relative error of at most 0.000071.
Values sent between devices are 32-bit elements; how exact they have to be, the bound alone decides.
A program may use at most 128 MiB of HBM per device.

v0:
```python
import jax
import jax.numpy as jnp
from jax import lax
from jax.sharding import PartitionSpec as P


def basis_table(count):
    rank = jnp.arange(count)
    angle = (
        jnp.pi
        / (count + 1)
        * ((rank[:, None] + 1) * (rank[None, :] + 1) % (2 * count + 2)).astype(jnp.float32)
    )
    return jnp.sin(angle) * (2.0 / (count + 1)) ** 0.5


def along_dim(values, dim):
    moved = jnp.tensordot(
        values, basis_table(values.shape[dim]), axes=([dim], [0]), precision=lax.Precision.HIGHEST
    )
    return jnp.moveaxis(moved, -1, dim)


def on_device(source, symbol_x, symbol_y, symbol_z):
    part_values = source
    part_values = along_dim(part_values, 0)
    part_values = lax.slice_in_dim(part_values, 0, part_values.shape[0] // 2, axis=0)
    part_values = lax.all_to_all(part_values, "north", split_axis=0, concat_axis=1, tiled=True)
    part_values = along_dim(part_values, 1)
    pencil_values = lax.slice_in_dim(part_values, 0, part_values.shape[1] // 2, axis=1)
    pencil_values = lax.all_to_all(pencil_values, "deep", split_axis=1, concat_axis=2, tiled=True)
    pencil_values = along_dim(pencil_values, 2)
    pencil_values = lax.slice_in_dim(pencil_values, 0, pencil_values.shape[2] // 2, axis=2)
    share_x = pencil_values.shape[0]
    part_x = lax.dynamic_slice_in_dim(symbol_x, lax.axis_index("north") * share_x, share_x)
    share_y = pencil_values.shape[1]
    part_y = lax.dynamic_slice_in_dim(symbol_y, lax.axis_index("deep") * share_y, share_y)
    symbol = (
        part_x[:, None, None]
        + part_y[None, :, None]
        + symbol_z[: pencil_values.shape[2]][None, None, :]
    )
    pencil_values = pencil_values * lax.rsqrt(symbol)
    return pencil_values


def solution(mesh):
    in_specs = (P(None, "north", "deep"), P(), P(), P())
    out_specs = P("north", "deep", None)
    return jax.shard_map(
        on_device, mesh=mesh, in_specs=in_specs, out_specs=out_specs, check_vma=False
    )
```

profile of v0, /device:TPU:1, one launch (start us, length us, event | category | flops | bytes accessed | tf_op | source)
XLA Modules:
  0.0 273.1 jit_solution(7118543344296502034)
XLA Ops:
  0.0 4.0 %fusion.18 = f32[512,512,1]{1,0,2:T(8,128)S(1)} fusion(s32[512]{0:T(512)S(1)} %iota_add_fusion.1), kind=kLoop, calls=%fused_computation.21 | loop fusion | flops 2621440 | bytes 1050624 | tf_op jit(solution)/shard_map/mul | solution.py:14
  4.1 24.3 %fusion.5 = f32[256,16,512]{2,0,1:T(8,128)S(1)} fusion(f32[512,16,512]{2,1,0:T(8,128)} %param.4, f32[512,512,1]{1,0,2:T(8,128)S(1)} %fusion.18), kind=kOutput, calls=%fused_computation.6 | convolution fusion | flops 12884901888 | bytes 25690112 | tf_op jit(solution)/shard_map/dot_general | solution.py:18
  28.3 4.9 %copy.24 = f32[256,16,512]{2,1,0:T(8,128)S(1)} copy(f32[256,16,512]{2,0,1:T(8,128)S(1)} %fusion.5) | data formatting | bytes 16777216 | tf_op jit(solution)/shard_map/slice | solution.py:27
  33.2 105.1 %all_to_all.36 = f32[256,16,512]{2,1,0:T(8,128)} all-to-all(f32[256,16,512]{2,1,0:T(8,128)S(1)} %copy.24), channel_id=1, replica_groups=mesh['north'=32,'deep'=4] {'north'}, dimensions={0} | all-to-all | bytes 16777216 | tf_op jit(solution)/shard_map/all_to_all | solution.py:28
  138.2 4.4 %copy.25 = f32[8,32,16,512]{3,2,1,0:T(8,128)S(1)} copy(f32[8,32,16,512]{3,2,0,1:T(8,128)} %bitcast.18) | data formatting | bytes 16777216 | tf_op jit(solution)/shard_map/all_to_all | solution.py:28
  142.7 18.9 %convolution_bitcast_fusion = f32[8,512,512]{1,2,0:T(8,128)S(1)} fusion(f32[8,512,512]{2,1,0:T(8,128)S(1)} %bitcast.17, s32[512]{0:T(512)S(1)} %iota_add_fusion.1), kind=kOutput, calls=%fused_computation.14 | convolution fusion | flops 12887523328 | bytes 16779264 | tf_op jit(solution)/shard_map/dot_general | solution.py:18
  161.6 2.5 slice.19
  164.1 5.6 %copy.27 = f32[8,256,512]{2,0,1:T(8,128)} copy(f32[8,256,512]{1,2,0:T(8,128)} %slice.19) | data formatting | bytes 8388608 | tf_op jit(solution)/shard_map/slice | solution.py:30
  169.7 5.0 %all-to-all-start.1 = ((f32[8,256,512]{2,0,1:T(8,128)}), f32[8,256,512]{2,0,1:T(8,128)}, u32[]{:S(2)}, u32[]{:S(2)}) async-start(f32[8,256,512]{2,0,1:T(8,128)} %copy.27), calls=%async_computation.1 | async-start | bytes 8388608 | tf_op jit(solution)/shard_map/all_to_all | solution.py:31
  174.7 0.8 dynamic_slice.7
  175.4 0.8 dynamic_slice.6
  176.2 0.1 broadcast_add_fusion
  176.3 65.8 %fusion.4 = f32[2048,2048,1]{1,0,2:T(8,128)} fusion(s32[2048]{0:T(1024)S(1)} %iota_add_fusion), kind=kLoop, calls=%fused_computation.5 | loop fusion | flops 41943040 | bytes 16785408 | tf_op jit(solution)/shard_map/mul | solution.py:14
  242.1 0.0 all-to-all-done.1
  242.1 0.0 slice-start
  242.1 6.9 %copy.29 = f32[8,64,4,512]{3,2,1,0:T(4,128)} copy(f32[8,64,4,512]{3,0,1,2:T(8,128)} %bitcast.8) | data formatting | bytes 8388608 | tf_op jit(solution)/shard_map/all_to_all | solution.py:31
  248.9 6.1 %all_to_all.33 = f32[8,64,2048]{2,1,0:T(8,128)} reshape(f32[8,64,4,512]{3,2,1,0:T(4,128)} %copy.29) | data formatting | bytes 8388608 | tf_op jit(solution)/shard_map/all_to_all | solution.py:31
  255.0 0.0 slice-done
  255.0 17.9 %rsqrt_multiply_fusion = f32[8,64,1024]{2,1,0:T(8,128)} fusion(f32[8,64,2048]{2,1,0:T(8,128)} %all_to_all.33, f32[2048,2048,1]{1,0,2:T(8,128)} %fusion.4, f32[1024]{0:T(1024)S(1)} %slice-done, f32[8,64]{1,0:T(8,128)S(1)} %broadcast_add_fusion), kind=kOutput, calls=%fused_computation.15 | convolution fusion | flops 12885950464 | bytes 14686208 | tf_op jit(solution)/shard_map/dot_general | solution.py:18
  (2 shorter events, 0.0 us)
Async XLA Ops:
  169.7 72.4 %all-to-all-start.1 = ((f32[8,256,512]{2,0,1:T(8,128)}), f32[8,256,512]{2,0,1:T(8,128)}, u32[]{:S(2)}, u32[]{:S(2)}) async-start(f32[8,256,512]{2,0,1:T(8,128)} %copy.27), calls=%async_computation.1 | async-start | bytes 8388608 | tf_op jit(solution)/shard_map/all_to_all | solution.py:31
  242.1 12.9 %slice-start = ((f32[2048]{0:T(1024)}), f32[1024]{0:T(1024)S(1)}, s32[]{:S(2)}) async-start(f32[2048]{0:T(1024)} %param.7), calls=%async_computation.2 | async-start | bytes 8192 | tf_op jit(solution)/shard_map/slice | solution.py:41
where the time goes:
time: 277 us; the launch traced here: 273 us
  blocking collectives  105 us (38%)
  other arithmetic  69.9 us (25%)
  matrix products  61.1 us (22%)
  local copies, waits for them, and re-layouts  31.8 us (11%)
  starting transfers between devices  5.01 us (2%)
    all_to_all x1, blocking collectives, on_device(): lax.all_to_all(part_values, 'north', split_axis=0, concat_axis=1, tiled=T...  105 us
    mul x2, other arithmetic, basis_table(): return jnp.sin(angle) * (2.0 / (count + 1)) ** 0.5  69.9 us
    dot_general x3, matrix products, along_dim(): jnp.tensordot(values, basis_table(values.shape[dim]), axes=([dim], [0]),...  61.1 us
    all_to_all x2, local copies, waits for them, and re-layouts, on_device(): lax.all_to_all(pencil_values, 'deep', split_axis=1, concat_axis=2, tiled=...  12.9 us
    slice x2, local copies, waits for them, and re-layouts, on_device(): lax.slice_in_dim(part_values, 0, part_values.shape[1] // 2, axis=1)  8.03 us
  transfers between devices with their start and end apart: 1, of which 0 were waited for; matrix products, arithmetic and copies ran while one was open for 25% of the time, Pallas kernels for 0%

commit v1 on v0

v1 whole, which is shorter than its diff:
```python
import functools

import jax
import jax.numpy as jnp
import numpy as np
from jax import lax
from jax.experimental import pallas as pl
from jax.experimental.pallas import tpu as pltpu
from jax.sharding import PartitionSpec as P

NORTH, DEEP = 32, 4
MESH = pl.DeviceIdType.MESH
F32, BF16 = jnp.float32, jnp.bfloat16


def split(values):
    high = values.astype(BF16)
    return high, (values - high.astype(F32)).astype(BF16)


def dot3(a_high, a_low, b_high, b_low):
    dot = functools.partial(jnp.dot, preferred_element_type=F32)
    return dot(a_high, b_high) + dot(a_low, b_high) + dot(a_high, b_low)


def peer_order():
    far = [0, 1, 2, 1]
    offsets = [(a, b, c) for a in range(4) for b in range(4) for c in range(2)]
    offsets.remove((0, 0, 0))
    return sorted(offsets, key=lambda o: (-(far[o[0]] + far[o[1]]), o[2], o[0], o[1]))


def kernel(
    source, table_high, table_low, fine, coarse, sym_x, sym_y, sym_z, out,
    planes, first, gath_a, gath_b, half_a, recv_a, half_b, recv_b, last_b, out_a,
    z_high, z_low, left_high, left_low, col_y,
    load_sem, na_send, na_recv, y1_send, y1_recv, y2_send, y2_recv,
    nb_send, nb_recv, y3_send, y3_recv, put_sem,
):
    n = lax.axis_index("north")
    d = lax.axis_index("deep")
    z_pos, x_pos, core = n // 8, (n // 2) % 4, n % 2

    def peer(offset):
        a, b, c = offset
        return ((z_pos + a) % 4) * 8 + ((x_pos + b) % 4) * 2 + (core + c) % 2

    barrier = pltpu.get_barrier_semaphore()
    for offset in peer_order():
        pl.semaphore_signal(barrier, inc=1, device_id=(peer(offset), d), device_id_type=MESH)
    for e in range(1, DEEP):
        pl.semaphore_signal(barrier, inc=1, device_id=(n, (d + e) % 4), device_id_type=MESH)

    def load(y):
        return pltpu.make_async_copy(source.at[:, y, :], planes.at[y], load_sem.at[y])

    for y in range(16):
        load(y).start()

    def wait_bytes(ref, sem):
        pltpu.make_async_copy(ref, ref, sem).wait()

    flat = first.reshape(4 * 256 * 16, 128)

    def x_step(y, _):
        load(y).wait()
        for half in range(2):
            high, low = split(planes[y, :, half * 256 : half * 256 + 256])
            res = dot3(table_high[...], table_low[...], high, low)
            for c in range(2):
                for m in range(NORTH):
                    row = (half * 2 + c) * 4096 + m * 128
                    flat[pl.ds(row + y, 8, stride=16), :] = res[
                        m * 8 : m * 8 + 8, c * 128 : c * 128 + 128
                    ]
        return 0

    lax.fori_loop(0, 16, x_step, 0)

    pl.semaphore_wait(barrier, NORTH - 1 + DEEP - 1)

    modes = first.reshape(4, 8, 4, 8, 16, 128)

    for s in range(4):
        g = (n + s) % 4
        for e in range(1, DEEP):
            to = (d + e) % 4
            pltpu.make_async_remote_copy(
                modes.at[:, :, g, 4 + to],
                gath_b.at[s, d],
                y1_send,
                y1_recv.at[s],
                device_id=(n, to),
                device_id_type=MESH,
            ).start()
        for offset in peer_order():
            to = peer(offset)
            pltpu.make_async_remote_copy(
                first.at[s, pl.ds(8 * to, 4)],
                gath_a.at[s, :, pl.ds(16 * n, 16)],
                na_send,
                na_recv.at[s],
                device_id=(to, d),
                device_id_type=MESH,
            ).start()

    for s in range(4):
        g = (n + s) % 4
        gath_a[s, :, pl.ds(16 * n, 16)] = first[s, pl.ds(8 * n, 4)]
        gath_b[s, d] = modes[:, :, g, 4 + d]

    fine_sin, fine_cos = fine.at[0], fine.at[1]

    def table_step(p, _):
        for q in range(2):
            cols = slice(q * 512, q * 512 + 512)
            sin_p = coarse[0, pl.ds(p, 1), cols]
            cos_p = coarse[1, pl.ds(p, 1), cols]

            def rows_step(r, _):
                rows = pl.ds(pl.multiple_of(r * 16, 16), 16)
                values = sin_p * fine_cos[rows, cols] + cos_p * fine_sin[rows, cols]
                high, low = split(values)
                to = pl.ds(pl.multiple_of(p * 128 + r * 16, 16), 16)
                z_high[to, cols] = high
                z_low[to, cols] = low
                return 0

            lax.fori_loop(0, 8, rows_step, 0)
        return 0

    lax.fori_loop(0, 16, table_step, 0)

    row_id = lax.broadcasted_iota(jnp.int32, (128, 128), 0)
    col_id = lax.broadcasted_iota(jnp.int32, (128, 128), 1)
    for h in range(2):
        picked = jnp.where(row_id == col_id, sym_y[0:1, h * 128 : h * 128 + 128], 0.0)
        col_y[h * 128 : h * 128 + 128, :] = jnp.broadcast_to(
            jnp.sum(picked, axis=1, keepdims=True), (128, 128)
        )

    def z_stage(load_block, rows, store):
        for b in range(16):
            high, low = split(load_block(b))
            left_high[0:rows, b * 128 : b * 128 + 128] = high
            left_low[0:rows, b * 128 : b * 128 + 128] = low

        def col_step(t, _):
            cols = pl.ds(pl.multiple_of(t * 256, 256), 256)
            res = dot3(
                left_high[0:rows, :], left_low[0:rows, :], z_high[:, cols], z_low[:, cols]
            )
            store(t, cols, res)
            return 0

        lax.fori_loop(0, 4, col_step, 0)

    def send_half_b(s, h):
        g = (n + s) % 4
        for r in range(8):
            mem = (n // 4 + 4 + r) % 8
            to = 4 * mem + g

            @pl.when(to != n)
            def _():
                pltpu.make_async_remote_copy(
                    half_b.at[h, s, mem],
                    recv_b.at[h, pl.ds(16 * n, 16)],
                    nb_send,
                    nb_recv.at[h],
                    device_id=(to, d),
                    device_id_type=MESH,
                ).start()

    def middle_step(s, _):
        wait_bytes(gath_a.at[s, :, pl.ds(0, 496)], na_recv.at[s])
        for pair in range(2):
            high, low = split(
                jnp.concatenate([gath_a[s, 2 * pair], gath_a[s, 2 * pair + 1]], axis=1)
            )
            res = dot3(table_high[...], table_low[...], high, low)
            half_a[s, 2 * pair] = res[:, :128]
            half_a[s, 2 * pair + 1] = res[:, 128:]
        for e in range(1, DEEP):
            to = (d + e) % 4
            pltpu.make_async_remote_copy(
                half_a.at[s, :, pl.ds(64 * to, 64)],
                recv_a.at[d, s],
                y2_send,
                y2_recv,
                device_id=(n, to),
                device_id_type=MESH,
            ).start()
        recv_a[d, s] = half_a[s, :, pl.ds(64 * d, 64)]

        wait_bytes(gath_b.at[s, pl.ds(0, 3)], y1_recv.at[s])

        def store(t, cols, res):
            half_b[t // 2, s, :, :, pl.ds(pl.multiple_of((t % 2) * 256, 256), 256)] = (
                res.reshape(8, 16, 256)
            )

        z_stage(lambda b: gath_b[s, b // 4, b % 4].reshape(128, 128), 128, store)
        send_half_b(s, 0)
        return 0

    lax.fori_loop(0, 4, middle_step, 0)
    lax.fori_loop(0, 4, lambda s, c: (send_half_b(s, 1), c)[1], 0)

    for h in range(2):
        recv_b[h, pl.ds(16 * n, 16)] = half_b[h, 0, n // 4]

    def half_step(h, _):
        wait_bytes(recv_b.at[h, pl.ds(0, 496)], nb_recv.at[h])
        for q in range(2):
            cols = slice(q * 256, q * 256 + 256)
            high, low = split(recv_b[h, :, cols])
            res = dot3(table_high[...], table_low[...], high, low)
            at = pl.ds(pl.multiple_of(h * 512 + q * 256, 256), 256)
            symbol = (sym_x[8 * n + 4 + d] + col_y[:, 0:1]) + sym_z[0:1, at]
            last_b[h, :, cols] = res * lax.rsqrt(symbol)
        for e in range(1, DEEP):
            to = (d + e) % 4
            pltpu.make_async_remote_copy(
                last_b.at[h, pl.ds(64 * to, 64)],
                out.at[4 + d, :, pl.ds(pl.multiple_of(h * 512, 512), 512)],
                y3_send,
                y3_recv,
                device_id=(n, to),
                device_id_type=MESH,
            ).start()
        put_b(h).start()
        return 0

    def put_b(h):
        return pltpu.make_async_copy(
            last_b.at[h, pl.ds(64 * d, 64)],
            out.at[4 + d, :, pl.ds(pl.multiple_of(h * 512, 512), 512)],
            put_sem.at[h],
        )

    lax.fori_loop(0, 2, half_step, 0)

    wait_bytes(recv_a.at[pl.ds(0, 3)], y2_recv)

    def store_a(t, cols, res):
        for i in range(4):
            symbol = (sym_x[8 * n + i] + col_y[pl.ds(64 * d, 64), 0:1]) + sym_z[0:1, cols]
            out_a[i, :, cols] = res[i * 64 : i * 64 + 64] * lax.rsqrt(symbol)

    z_stage(lambda b: recv_a[b // 4, b % 4].reshape(256, 128), 256, store_a)
    put_a = pltpu.make_async_copy(out_a, out.at[pl.ds(0, 4)], put_sem.at[2])
    put_a.start()

    wait_bytes(first.at[:, pl.ds(0, 124)], na_send)
    wait_bytes(gath_b.at[:, pl.ds(0, 3)], y1_send)
    wait_bytes(recv_a.at[pl.ds(0, 3)], y2_send)
    wait_bytes(recv_b.at[:, pl.ds(0, 496)], nb_send)
    wait_bytes(last_b.at[:, pl.ds(0, 192)], y3_send)
    for h in range(2):
        put_b(h).wait()
    put_a.wait()
    wait_bytes(last_b.at[:, pl.ds(0, 192)], y3_recv)


def tables():
    count = 512
    rank = np.arange(count, dtype=np.int64)
    angle = np.pi / (count + 1) * (((rank[:256, None] + 1) * (rank[None, :] + 1)) % (2 * count + 2))
    table = np.sin(angle) * np.sqrt(2.0 / (count + 1))
    table = table.astype(np.float32)
    high = table.astype(BF16)
    low = (table - high.astype(np.float32)).astype(BF16)
    count = 2048
    rank = np.arange(1024, dtype=np.int64)[None, :] + 1
    step = np.pi / (count + 1)
    fine = step * ((np.arange(128, dtype=np.int64)[:, None] * rank) % (2 * count + 2))
    coarse = step * (((128 * np.arange(16, dtype=np.int64)[:, None] + 1) * rank) % (2 * count + 2))
    gain = np.sqrt(2.0 / (count + 1))
    fine = np.stack([np.sin(fine), np.cos(fine)]).astype(np.float32)
    coarse = (gain * np.stack([np.sin(coarse), np.cos(coarse)])).astype(np.float32)
    return high, low, fine, coarse


def on_device(source, symbol_x, symbol_y, symbol_z):
    high, low, fine, coarse = tables()
    vmem = pl.BlockSpec(memory_space=pltpu.VMEM)
    anywhere = pl.BlockSpec(memory_space=pl.ANY)
    dma = pltpu.SemaphoreType.DMA
    return pl.pallas_call(
        kernel,
        out_shape=jax.ShapeDtypeStruct((8, 64, 1024), F32),
        in_specs=[anywhere, vmem, vmem, vmem, vmem]
        + [pl.BlockSpec(memory_space=pltpu.SMEM), vmem, vmem],
        out_specs=anywhere,
        scratch_shapes=[
            pltpu.VMEM((16, 512, 512), F32),
            pltpu.VMEM((4, 256, 16, 128), F32),
            pltpu.VMEM((4, 4, 512, 128), F32),
            pltpu.VMEM((4, 4, 4, 8, 16, 128), F32),
            pltpu.VMEM((4, 4, 256, 128), F32),
            pltpu.VMEM((4, 4, 4, 64, 128), F32),
            pltpu.VMEM((2, 4, 8, 16, 512), F32),
            pltpu.VMEM((2, 512, 512), F32),
            pltpu.VMEM((2, 256, 512), F32),
            pltpu.VMEM((4, 64, 1024), F32),
            pltpu.VMEM((2048, 1024), BF16),
            pltpu.VMEM((2048, 1024), BF16),
            pltpu.VMEM((256, 2048), BF16),
            pltpu.VMEM((256, 2048), BF16),
            pltpu.VMEM((256, 128), F32),
            dma((16,)),
            dma,
            dma((4,)),
            dma,
            dma((4,)),
            dma,
            dma,
            dma,
            dma((2,)),
            dma,
            dma,
            dma((3,)),
        ],
        compiler_params=pltpu.CompilerParams(
            collective_id=0, has_side_effects=True, vmem_limit_bytes=63 << 20
        ),
    )(
        source,
        high,
        low,
        fine,
        coarse,
        symbol_x,
        symbol_y.reshape(1, 512),
        symbol_z.reshape(1, 2048),
    )


def solution(mesh):
    in_specs = (P(None, "north", "deep"), P(), P(), P())
    out_specs = P("north", "deep", None)
    return jax.shard_map(
        on_device, mesh=mesh, in_specs=in_specs, out_specs=out_specs, check_vma=False
    )
```

time: 277 us -> 105 us (0.38); the launches traced: 273 us -> 105 us
  blocking collectives: 105 us -> 0 us
  Pallas kernels: 0 us -> 101 us
  other arithmetic: 69.9 us -> 0 us
  matrix products: 61.1 us -> 0 us
  local copies, waits for them, and re-layouts: 31.8 us -> 3.16 us
  starting transfers between devices: 5.01 us -> 0 us
    all_to_all x1 -> x0, blocking collectives: 105 us -> none  [on_device(): lax.all_to_all(part_values, 'north', split_axis=0, concat_axis=1, tiled=T...]
    pallas_call x0 -> x1, Pallas kernels: none -> 101 us  [on_device(): pl.pallas_call(kernel, out_shape=jax.ShapeDtypeStruct((8, 64, 1024), F32)...]
    mul x2 -> x0, other arithmetic: 69.9 us -> none  [basis_table(): return jnp.sin(angle) * (2.0 / (count + 1)) ** 0.5]
    dot_general x3 -> x0, matrix products: 61.1 us -> none  [along_dim(): jnp.tensordot(values, basis_table(values.shape[dim]), axes=([dim], [0]),...]
    all_to_all x3 -> x0, local copies, waits for them, and re-layouts: 17.4 us -> none  [the longest x2 12.9 us: on_device(): lax.all_to_all(pencil_values, 'deep', split_axis=1, concat_axis=2, tiled=...]
    slice x5 -> x0, local copies, waits for them, and re-layouts: 12.9 us -> none  [the longest x2 8.03 us: on_device(): lax.slice_in_dim(part_values, 0, part_values.shape[1] // 2, axis=1)]
    all_to_all x1 -> x0, starting transfers between devices: 5.01 us -> none  [on_device(): lax.all_to_all(pencil_values, 'deep', split_axis=1, concat_axis=2, tiled=...]
    unnamed x0 -> x1, local copies, waits for them, and re-layouts: none -> 3.16 us
  transfers between devices with their start and end apart: 1 -> 0, of which waited for: 0 -> 0; matrix products, arithmetic and copies ran while one was open for 25% -> 0% of each run, Pallas kernels for 0% -> 0%
where the time goes in v1:
time: 105 us
  Pallas kernels  101 us (96%)
  local copies, waits for them, and re-layouts  3.16 us (3%)
    pallas_call x1, Pallas kernels, on_device(): pl.pallas_call(kernel, out_shape=jax.ShapeDtypeStruct((8, 64, 1024), F32)...  101 us
    unnamed x1, local copies, waits for them, and re-layouts  3.16 us

profile of v1, /device:TPU:1, one launch (start us, length us, event | category | flops | bytes accessed | tf_op | source)
XLA Modules:
  0.0 104.5 jit_solution(2041185778335684952)
XLA Ops:
  0.0 101.4 %shard_map.82 = f32[8,64,1024]{2,1,0:T(8,128)} custom-call(f32[512,16,512]{2,1,0:T(8,128)} %source.1, bf16[256,512]{1,0:T(8,128)(2,1)} %constant.8.clone.table_high, bf16[256,512]{1,0:T(8,128)(2,1)} %constant.9.clone.table_low, f32[2,128,1024]{2,1,0:T(8,128)} %constant.10.clone.fine, f32[2,16,1024]{2,1,0:T(8,128)} %constant.11.clone.coarse, f32[512]{0:T(512)} %sym_x.1, ...), custom_call_target="tpu_custom_call" | custom-call | tf_op jit(solution)/shard_map/pallas_call | solution.py:290
  101.4 3.2 %copy.10 = f32[8,64,1024]{2,1,0:T(8,128)} copy(f32[8,64,1024]{2,1,0:T(8,128)} %shard_map.82) | data formatting | bytes 4194304

commit v2 on v1

v2 whole, which is shorter than its diff:
```python
import functools

import jax
import jax.numpy as jnp
import numpy as np
from jax import lax
from jax.experimental import pallas as pl
from jax.experimental.pallas import tpu as pltpu
from jax.sharding import PartitionSpec as P

NORTH, DEEP = 32, 4
CHUNKS, WIDE = 4, 2
MESH = pl.DeviceIdType.MESH
F32, BF16 = jnp.float32, jnp.bfloat16


def split(values):
    high = values.astype(BF16)
    return high, (values - high.astype(F32)).astype(BF16)


def dot3(a_high, a_low, b_high, b_low):
    dot = functools.partial(jnp.dot, preferred_element_type=F32)
    return dot(a_high, b_high) + dot(a_low, b_high) + dot(a_high, b_low)


def peer_order():
    far = [0, 1, 2, 1]
    offsets = [(a, b, c) for a in range(4) for b in range(4) for c in range(2)]
    offsets.remove((0, 0, 0))
    return sorted(offsets, key=lambda o: (-(far[o[0]] + far[o[1]]), o[2], o[0], o[1]))


def wait_bytes(ref, sem):
    pltpu.make_async_copy(ref, ref, sem).wait()


def kernel(
    source, x_hbm, y_hbm, fine_hbm, coarse_hbm, sym_x_hbm, sym_y_hbm, sym_z_hbm, out,
    planes, x_tab, y_tab, fine, coarse, sym_x, sym_y, sym_z, first_a, first_b, gath_a, gath_b, half_a, recv_a,
    half_b, recv_b, last_b, z_high, z_low, left_high, left_low, col_y,
    load_sem, tab_sem, na_send, na_recv, y1_send, y1_recv, y2_send, y2_recv,
    nb_send, nb_recv, y3_send, y3_recv,
):
    n = lax.axis_index("north")
    d = lax.axis_index("deep")
    z_pos, x_pos, core = n // 8, (n // 2) % 4, n % 2

    def place(offset):
        a, b, c = offset
        return (z_pos + a) % 4, (x_pos + b) % 4, (core + c) % 2

    def peer(offset):
        a, b, c = place(offset)
        return a * 8 + b * 2 + c

    barrier = pltpu.get_barrier_semaphore()
    for offset in peer_order():
        pl.semaphore_signal(barrier, inc=1, device_id=(peer(offset), d), device_id_type=MESH)
    for e in range(1, DEEP):
        pl.semaphore_signal(barrier, inc=1, device_id=(n, (d + e) % 4), device_id_type=MESH)

    tabs = [
        pltpu.make_async_copy(a, b, tab_sem.at[i])
        for i, (a, b) in enumerate(
            [
                (x_hbm, x_tab),
                (y_hbm, y_tab),
                (fine_hbm, fine),
                (coarse_hbm, coarse),
                (sym_x_hbm, sym_x),
                (sym_y_hbm, sym_y),
                (sym_z_hbm, sym_z),
            ]
        )
    ]

    def load(y):
        return pltpu.make_async_copy(source.at[:, y, :], planes.at[y], load_sem.at[y])

    tabs[0].start()
    for y in range(16):
        load(y).start()
    for tab in tabs[1:]:
        tab.start()
    tabs[0].wait()

    flat_a = first_a.reshape(4 * 128 * 16, 128)

    def x_step(pair, _):
        for j in range(2):
            load(2 * pair + j).wait()
        for j in range(2):
            y = 2 * pair + j
            for half in range(2):
                high, low = split(planes[y, :, half * 256 : half * 256 + 256])
                res = dot3(x_tab[0], x_tab[1], high, low)
                for c in range(2):
                    cols = slice(c * 128, c * 128 + 128)
                    zc = half * 2 + c
                    for m in range(16):
                        row = (zc * 128 + m * 8) * 16
                        flat_a[pl.ds(row + y, 8, stride=16), :] = res[m * 8 : m * 8 + 8, cols]
                    first_b[zc, y] = res[128:, cols].reshape(4, 32, 128)
        return 0

    def send_first_b(q, _):
        for e in range(1, DEEP):
            to = (d + e) % 4
            pltpu.make_async_remote_copy(
                first_b.at[:, pl.ds(4 * q, 4), to],
                gath_b.at[q, d],
                y1_send,
                y1_recv.at[q],
                device_id=(n, to),
                device_id_type=MESH,
            ).start()
        return 0

    lax.fori_loop(0, 6, x_step, 0)
    pl.semaphore_wait(barrier, NORTH - 1 + DEEP - 1)
    lax.fori_loop(0, 3, send_first_b, 0)
    lax.fori_loop(6, 8, x_step, 0)
    send_first_b(3, 0)

    def send_a(s, _):
        for offset in peer_order():
            to = peer(offset)
            pltpu.make_async_remote_copy(
                first_a.at[s, pl.ds(4 * to, 4)],
                gath_a.at[s, :, pl.ds(16 * n, 16)],
                na_send,
                na_recv.at[s],
                device_id=(to, d),
                device_id_type=MESH,
            ).start()
        return 0

    lax.fori_loop(0, 4, send_a, 0)

    for s in range(4):
        gath_a[s, :, pl.ds(16 * n, 16)] = first_a[s, pl.ds(4 * n, 4)]
        gath_b[s, d] = first_b[:, pl.ds(4 * s, 4), d]

    for tab in tabs[1:]:
        tab.wait()

    def table_step(p, _):
        for q in range(2):
            cols = slice(q * 512, q * 512 + 512)
            sin_p = coarse[0, pl.ds(p, 1), cols]
            cos_p = coarse[1, pl.ds(p, 1), cols]

            def rows_step(r, _):
                rows = pl.ds(pl.multiple_of(r * 16, 16), 16)
                values = sin_p * fine[1, rows, cols] + cos_p * fine[0, rows, cols]
                high, low = split(values)
                to = pl.ds(pl.multiple_of(p * 128 + r * 16, 16), 16)
                z_high[to, cols] = high
                z_low[to, cols] = low
                return 0

            lax.fori_loop(0, 8, rows_step, 0)
        return 0

    lax.fori_loop(0, 16, table_step, 0)

    row_id = lax.broadcasted_iota(jnp.int32, (128, 128), 0)
    col_id = lax.broadcasted_iota(jnp.int32, (128, 128), 1)
    for h in range(2):
        picked = jnp.where(row_id == col_id, sym_y[0:1, h * 128 : h * 128 + 128], 0.0)
        col_y[h * 128 : h * 128 + 128, :] = jnp.broadcast_to(
            jnp.sum(picked, axis=1, keepdims=True), (128, 128)
        )

    def z_stage(load_block, rows, store):
        for b in range(16):
            high, low = split(load_block(b))
            left_high[0:rows, b * 128 : b * 128 + 128] = high
            left_low[0:rows, b * 128 : b * 128 + 128] = low

        def col_step(t, _):
            cols = pl.ds(pl.multiple_of(t * 256, 256), 256)
            res = dot3(
                left_high[0:rows, :], left_low[0:rows, :], z_high[:, cols], z_low[:, cols]
            )
            store(t, cols, res)
            return 0

        lax.fori_loop(0, 4, col_step, 0)

    def step_a(s):
        wait_bytes(gath_a.at[s, :, pl.ds(0, 496)], na_recv.at[s])
        for i in range(0, 4, 2):
            high, low = split(jnp.concatenate([gath_a[s, i], gath_a[s, i + 1]], axis=1))
            res = dot3(y_tab[0], y_tab[1], high, low)
            half_a[s, i] = res[:, :128]
            half_a[s, i + 1] = res[:, 128:]
        for e in range(1, DEEP):
            to = (d + e) % 4
            pltpu.make_async_remote_copy(
                half_a.at[s, :, pl.ds(64 * to, 64)],
                recv_a.at[d, s],
                y2_send,
                y2_recv,
                device_id=(n, to),
                device_id_type=MESH,
            ).start()
        recv_a[d, s] = half_a[s, :, pl.ds(64 * d, 64)]

    flat_b = half_b.reshape(8 * 32 * 16, 128)

    def step_b(q):
        wait_bytes(gath_b.at[q, pl.ds(0, 3)], y1_recv.at[q])

        def store(t, cols, res):
            for c in range(2):
                for y in range(4):
                    for m in range(4):
                        at = y * 32 + m * 8
                        row = ((2 * t + c) * 32 + m * 8) * 16 + 4 * q + y
                        flat_b[pl.ds(row, 8, stride=16), :] = res[
                            at : at + 8, c * 128 : c * 128 + 128
                        ]

        z_stage(lambda b: gath_b[q, b // 4, b % 4].reshape(128, 128), 128, store)

    def middle_step(s, _):
        step_b(s)
        step_a(s)
        return 0

    lax.fori_loop(0, 3, middle_step, 0)
    step_b(3)

    def send_b(ch, _):
        for offset in peer_order():
            to = peer(offset)
            pltpu.make_async_remote_copy(
                half_b.at[pl.ds(WIDE * ch, WIDE), to],
                recv_b.at[pl.ds(WIDE * ch, WIDE), pl.ds(16 * n, 16)],
                nb_send,
                nb_recv.at[ch],
                device_id=(to, d),
                device_id_type=MESH,
            ).start()
        return 0

    lax.fori_loop(0, CHUNKS, send_b, 0)
    recv_b[:, pl.ds(16 * n, 16)] = half_b[:, n]
    step_a(3)

    def last_step(ch, _):
        wait_bytes(recv_b.at[pl.ds(WIDE * ch, WIDE), pl.ds(0, 496)], nb_recv.at[ch])
        cols = pl.ds(pl.multiple_of(ch * WIDE * 128, WIDE * 128), WIDE * 128)
        high, low = split(jnp.concatenate([recv_b[WIDE * ch + j] for j in range(WIDE)], axis=1))
        res = dot3(y_tab[0], y_tab[1], high, low)
        symbol = (sym_x[8 * n + 4 + d] + col_y[:, 0:1]) + sym_z[0:1, cols]
        last_b[:, cols] = res * lax.rsqrt(symbol)
        for e in range(1, DEEP):
            to = (d + e) % 4
            pltpu.make_async_remote_copy(
                last_b.at[pl.ds(64 * to, 64), cols],
                out.at[4 + d, :, cols],
                y3_send,
                y3_recv,
                device_id=(n, to),
                device_id_type=MESH,
            ).start()
        out[4 + d, :, cols] = last_b[pl.ds(64 * d, 64), cols]
        return 0

    lax.fori_loop(0, CHUNKS, last_step, 0)

    wait_bytes(recv_a.at[pl.ds(0, 3)], y2_recv)

    def store_a(t, cols, res):
        for i in range(4):
            symbol = (sym_x[8 * n + i] + col_y[pl.ds(64 * d, 64), 0:1]) + sym_z[0:1, cols]
            out[i, :, cols] = res[i * 64 : i * 64 + 64] * lax.rsqrt(symbol)

    z_stage(lambda b: recv_a[b // 4, b % 4].reshape(256, 128), 256, store_a)

    wait_bytes(first_a.at[:, pl.ds(0, 124)], na_send)
    wait_bytes(gath_b.at[:, pl.ds(0, 3)], y1_send)
    wait_bytes(recv_a.at[pl.ds(0, 3)], y2_send)
    wait_bytes(half_b.at[:, pl.ds(0, 31)], nb_send)
    wait_bytes(last_b.at[pl.ds(0, 192)], y3_send)
    wait_bytes(last_b.at[pl.ds(0, 192)], y3_recv)


def halves(table):
    table = table.astype(np.float32)
    high = table.astype(BF16)
    return np.stack([high, (table - high.astype(np.float32)).astype(BF16)])


def tables():
    count = 512
    rank = np.arange(count, dtype=np.int64)
    angle = np.pi / (count + 1) * (((rank[:256, None] + 1) * (rank[None, :] + 1)) % (2 * count + 2))
    table = np.sin(angle) * np.sqrt(2.0 / (count + 1))
    rows = [8 * n + i for n in range(NORTH) for i in range(4)]
    rows += [8 * n + 4 + e for e in range(DEEP) for n in range(NORTH)]
    count = 2048
    rank = np.arange(1024, dtype=np.int64)[None, :] + 1
    step = np.pi / (count + 1)
    fine = step * ((np.arange(128, dtype=np.int64)[:, None] * rank) % (2 * count + 2))
    coarse = step * (((128 * np.arange(16, dtype=np.int64)[:, None] + 1) * rank) % (2 * count + 2))
    gain = np.sqrt(2.0 / (count + 1))
    fine = np.stack([np.sin(fine), np.cos(fine)]).astype(np.float32)
    coarse = (gain * np.stack([np.sin(coarse), np.cos(coarse)])).astype(np.float32)
    return halves(table[rows]), halves(table), fine, coarse


def on_device(source, symbol_x, symbol_y, symbol_z):
    vmem = pl.BlockSpec(memory_space=pltpu.VMEM)
    anywhere = pl.BlockSpec(memory_space=pl.ANY)
    dma = pltpu.SemaphoreType.DMA
    return pl.pallas_call(
        kernel,
        out_shape=pltpu.VMEM((8, 64, 1024), F32),
        in_specs=[anywhere] * 8,
        out_specs=vmem,
        scratch_shapes=[
            pltpu.VMEM((16, 512, 512), F32),
            pltpu.VMEM((2, 256, 512), BF16),
            pltpu.VMEM((2, 256, 512), BF16),
            pltpu.VMEM((2, 128, 1024), F32),
            pltpu.VMEM((2, 16, 1024), F32),
            pltpu.SMEM((512,), F32),
            pltpu.VMEM((1, 512), F32),
            pltpu.VMEM((1, 2048), F32),
            pltpu.VMEM((4, 128, 16, 128), F32),
            pltpu.VMEM((4, 16, 4, 32, 128), F32),
            pltpu.VMEM((4, 4, 512, 128), F32),
            pltpu.VMEM((4, 4, 4, 4, 32, 128), F32),
            pltpu.VMEM((4, 4, 256, 128), F32),
            pltpu.VMEM((4, 4, 4, 64, 128), F32),
            pltpu.VMEM((8, 32, 16, 128), F32),
            pltpu.VMEM((8, 512, 128), F32),
            pltpu.VMEM((256, 1024), F32),
            pltpu.VMEM((2048, 1024), BF16),
            pltpu.VMEM((2048, 1024), BF16),
            pltpu.VMEM((256, 2048), BF16),
            pltpu.VMEM((256, 2048), BF16),
            pltpu.VMEM((256, 128), F32),
            dma((16,)),
            dma((7,)),
            dma,
            dma((4,)),
            dma,
            dma((4,)),
            dma,
            dma,
            dma,
            dma((CHUNKS,)),
            dma,
            dma,
        ],
        compiler_params=pltpu.CompilerParams(
            collective_id=0, has_side_effects=True, vmem_limit_bytes=60 << 20
        ),
    )(
        source,
        *tables(),
        symbol_x,
        symbol_y.reshape(1, 512),
        symbol_z.reshape(1, 2048),
    )


def solution(mesh):
    in_specs = (P(None, "north", "deep"), P(), P(), P())
    out_specs = P("north", "deep", None)
    return jax.shard_map(
        on_device, mesh=mesh, in_specs=in_specs, out_specs=out_specs, check_vma=False
    )
```

time: 105 us -> 97.4 us (0.928)
  Pallas kernels: 101 us -> 95.9 us
  local copies, waits for them, and re-layouts: 3.16 us -> 1.32 us
    pallas_call x1, Pallas kernels: 101 us -> 95.9 us  [on_device(): pl.pallas_call(kernel, out_shape=pltpu.VMEM((8, 64, 1024), F32), in_specs...]
    unnamed x1, local copies, waits for them, and re-layouts: 3.16 us -> 1.32 us
where the time goes in v2:
time: 97.4 us; the launch traced here: 97.3 us
  Pallas kernels  95.9 us (98%)
  local copies, waits for them, and re-layouts  1.32 us (1%)
    pallas_call x1, Pallas kernels, on_device(): pl.pallas_call(kernel, out_shape=pltpu.VMEM((8, 64, 1024), F32), in_specs...  95.9 us

profile of v2, /device:TPU:1, one launch (start us, length us, event | category | flops | bytes accessed | tf_op | source)
XLA Modules:
  0.0 97.3 jit_solution(842447991499879493)
XLA Ops:
  0.0 95.9 %shard_map.82 = f32[8,64,1024]{2,1,0:T(8,128)S(1)} custom-call(f32[512,16,512]{2,1,0:T(8,128)} %source.1, bf16[2,256,512]{2,1,0:T(8,128)(2,1)} %constant.8.clone.x_hbm, bf16[2,256,512]{2,1,0:T(8,128)(2,1)} %constant.9.clone.y_hbm, f32[2,128,1024]{2,1,0:T(8,128)} %constant.10.clone.fine_hbm, f32[2,16,1024]{2,1,0:T(8,128)} %constant.11.clone.coarse_hbm, ...), custom_call_target="tpu_custom_call" | custom-call | tf_op jit(solution)/shard_map/pallas_call | solution.py:320
  96.0 1.3 %copy.10 = f32[8,64,1024]{2,1,0:T(8,128)} copy(f32[8,64,1024]{2,1,0:T(8,128)S(1)} %shard_map.82) | data formatting | bytes 4194304

commit v3 on v2

--- a/solution.py
+++ b/solution.py
@@ -40,7 +40,7 @@
     planes, x_tab, y_tab, fine, coarse, sym_x, sym_y, sym_z, first_a, first_b, gath_a, gath_b, half_a, recv_a,
     half_b, recv_b, last_b, z_high, z_low, left_high, left_low, col_y,
     load_sem, tab_sem, na_send, na_recv, y1_send, y1_recv, y2_send, y2_recv,
-    nb_send, nb_recv, y3_send, y3_recv,
+    nb_send, nb_recv, y3_send, y3_recv, heard,
 ):
     n = lax.axis_index("north")
     d = lax.axis_index("deep")
@@ -55,10 +55,28 @@
         return a * 8 + b * 2 + c
 
     barrier = pltpu.get_barrier_semaphore()
+    partner = n + 1 - 2 * core
+
+    def tell(north, deep):
+        pl.semaphore_signal(barrier, inc=1, device_id=(north, deep), device_id_type=MESH)
+
     for offset in peer_order():
-        pl.semaphore_signal(barrier, inc=1, device_id=(peer(offset), d), device_id_type=MESH)
+        a, b, _ = place(offset)
+        if offset[2] == 0:
+            tell(a * 8 + b * 2 + 1, d)
     for e in range(1, DEEP):
-        pl.semaphore_signal(barrier, inc=1, device_id=(n, (d + e) % 4), device_id_type=MESH)
+        tell(n - core, (d + e) % 4)
+    tell(partner, d)
+
+    def ready(first_core, count):
+        @pl.when(core == first_core)
+        def _():
+            pl.semaphore_wait(barrier, count)
+            pl.semaphore_signal(heard, inc=1, device_id=(partner, d), device_id_type=MESH)
+
+        @pl.when(core != first_core)
+        def _():
+            pl.semaphore_wait(heard, 1)
 
     tabs = [
         pltpu.make_async_copy(a, b, tab_sem.at[i])
@@ -117,26 +135,36 @@
             ).start()
         return 0
 
-    lax.fori_loop(0, 6, x_step, 0)
-    pl.semaphore_wait(barrier, NORTH - 1 + DEEP - 1)
-    lax.fori_loop(0, 3, send_first_b, 0)
+    def send_first_a(half):
+        def body(s, _):
+            for offset in peer_order():
+                to = peer(offset)
+                pltpu.make_async_remote_copy(
+                    first_a.at[s, pl.ds(4 * to, 4), pl.ds(8 * half, 8)],
+                    gath_a.at[s, :, pl.ds(16 * n + 8 * half, 8)],
+                    na_send,
+                    na_recv.at[s],
+                    device_id=(to, d),
+                    device_id_type=MESH,
+                ).start()
+            return 0
+
+        lax.fori_loop(0, 4, body, 0)
+
+    def x_sends(q, _):
+        send_first_b(q, 0)
+        lax.fori_loop(2 * q + 2, 2 * q + 4, x_step, 0)
+        return 0
+
+    lax.fori_loop(0, 2, x_step, 0)
+    ready(0, 2 * (DEEP - 1) + 1)
+    lax.fori_loop(0, 2, x_sends, 0)
+    send_first_b(2, 0)
+    ready(1, NORTH - 1)
+    send_first_a(0)
     lax.fori_loop(6, 8, x_step, 0)
     send_first_b(3, 0)
-
-    def send_a(s, _):
-        for offset in peer_order():
-            to = peer(offset)
-            pltpu.make_async_remote_copy(
-                first_a.at[s, pl.ds(4 * to, 4)],
-                gath_a.at[s, :, pl.ds(16 * n, 16)],
-                na_send,
-                na_recv.at[s],
-                device_id=(to, d),
-                device_id_type=MESH,
-            ).start()
-        return 0
-
-    lax.fori_loop(0, 4, send_a, 0)
+    send_first_a(1)
 
     for s in range(4):
         gath_a[s, :, pl.ds(16 * n, 16)] = first_a[s, pl.ds(4 * n, 4)]
@@ -225,33 +253,37 @@
 
         z_stage(lambda b: gath_b[q, b // 4, b % 4].reshape(128, 128), 128, store)
 
-    def middle_step(s, _):
-        step_b(s)
-        step_a(s)
-        return 0
-
-    lax.fori_loop(0, 3, middle_step, 0)
-    step_b(3)
-
-    def send_b(ch, _):
+    def send_half_b(modes, half, sem):
         for offset in peer_order():
             to = peer(offset)
             pltpu.make_async_remote_copy(
-                half_b.at[pl.ds(WIDE * ch, WIDE), to],
-                recv_b.at[pl.ds(WIDE * ch, WIDE), pl.ds(16 * n, 16)],
+                half_b.at[modes, to, pl.ds(8 * half, 8)],
+                recv_b.at[modes, pl.ds(16 * n + 8 * half, 8)],
                 nb_send,
-                nb_recv.at[ch],
+                sem,
                 device_id=(to, d),
                 device_id_type=MESH,
             ).start()
-        return 0
-
-    lax.fori_loop(0, CHUNKS, send_b, 0)
+
+    def send_upper(ch, _):
+        send_half_b(pl.ds(WIDE * ch, WIDE), 1, nb_recv.at[ch])
+        return 0
+
+    def middle_step(s, _):
+        step_b(s)
+        step_a(2 * s - 4)
+        step_a(2 * s - 3)
+        return 0
+
+    lax.fori_loop(0, 2, lambda q, c: (step_b(q), c)[1], 0)
+    send_half_b(slice(None), 0, nb_recv.at[CHUNKS])
+    lax.fori_loop(2, 4, middle_step, 0)
+    lax.fori_loop(0, CHUNKS, send_upper, 0)
     recv_b[:, pl.ds(16 * n, 16)] = half_b[:, n]
-    step_a(3)
+    wait_bytes(recv_b.at[:, pl.ds(0, 248)], nb_recv.at[CHUNKS])
 
     def last_step(ch, _):
-        wait_bytes(recv_b.at[pl.ds(WIDE * ch, WIDE), pl.ds(0, 496)], nb_recv.at[ch])
+        wait_bytes(recv_b.at[pl.ds(WIDE * ch, WIDE), pl.ds(0, 248)], nb_recv.at[ch])
         cols = pl.ds(pl.multiple_of(ch * WIDE * 128, WIDE * 128), WIDE * 128)
         high, low = split(jnp.concatenate([recv_b[WIDE * ch + j] for j in range(WIDE)], axis=1))
         res = dot3(y_tab[0], y_tab[1], high, low)
@@ -354,9 +386,10 @@
             dma,
             dma,
             dma,
-            dma((CHUNKS,)),
-            dma,
-            dma,
+            dma((CHUNKS + 1,)),
+            dma,
+            dma,
+            pltpu.SemaphoreType.REGULAR,
         ],
         compiler_params=pltpu.CompilerParams(
             collective_id=0, has_side_effects=True, vmem_limit_bytes=60 << 20

time: 97.4 us -> 94.2 us (0.967)
  Pallas kernels: 95.9 us -> 92.7 us
    pallas_call x1, Pallas kernels: 95.9 us -> 92.7 us  [on_device(): pl.pallas_call(kernel, out_shape=pltpu.VMEM((8, 64, 1024), F32), in_specs...]
where the time goes in v3:
time: 94.2 us; the launch traced here: 94.1 us
  Pallas kernels  92.7 us (98%)
  local copies, waits for them, and re-layouts  1.32 us (1%)
    pallas_call x1, Pallas kernels, on_device(): pl.pallas_call(kernel, out_shape=pltpu.VMEM((8, 64, 1024), F32), in_specs...  92.7 us

profile of v3, /device:TPU:1, one launch (start us, length us, event | category | flops | bytes accessed | tf_op | source)
XLA Modules:
  0.0 94.1 jit_solution(6242553602266613416)
XLA Ops:
  0.0 92.7 %shard_map.82 = f32[8,64,1024]{2,1,0:T(8,128)S(1)} custom-call(f32[512,16,512]{2,1,0:T(8,128)} %source.1, bf16[2,256,512]{2,1,0:T(8,128)(2,1)} %constant.8.clone.x_hbm, bf16[2,256,512]{2,1,0:T(8,128)(2,1)} %constant.9.clone.y_hbm, f32[2,128,1024]{2,1,0:T(8,128)} %constant.10.clone.fine_hbm, f32[2,16,1024]{2,1,0:T(8,128)} %constant.11.clone.coarse_hbm, ...), custom_call_target="tpu_custom_call" | custom-call | tf_op jit(solution)/shard_map/pallas_call | solution.py:352
  92.8 1.3 %copy.10 = f32[8,64,1024]{2,1,0:T(8,128)} copy(f32[8,64,1024]{2,1,0:T(8,128)S(1)} %shard_map.82) | data formatting | bytes 4194304

commit v4 on v3

--- a/solution.py
+++ b/solution.py
@@ -9,7 +9,7 @@
 from jax.sharding import PartitionSpec as P
 
 NORTH, DEEP = 32, 4
-CHUNKS, WIDE = 4, 2
+CHUNKS, WIDE = 8, 1
 MESH = pl.DeviceIdType.MESH
 F32, BF16 = jnp.float32, jnp.bfloat16
 
@@ -158,10 +158,12 @@
 
     lax.fori_loop(0, 2, x_step, 0)
     ready(0, 2 * (DEEP - 1) + 1)
-    lax.fori_loop(0, 2, x_sends, 0)
-    send_first_b(2, 0)
+    lax.fori_loop(0, 1, x_sends, 0)
+    send_first_b(1, 0)
     ready(1, NORTH - 1)
     send_first_a(0)
+    lax.fori_loop(4, 6, x_step, 0)
+    send_first_b(2, 0)
     lax.fori_loop(6, 8, x_step, 0)
     send_first_b(3, 0)
     send_first_a(1)
@@ -276,7 +278,7 @@
         return 0
 
     lax.fori_loop(0, 2, lambda q, c: (step_b(q), c)[1], 0)
-    send_half_b(slice(None), 0, nb_recv.at[CHUNKS])
+    send_half_b(pl.ds(0, 8), 0, nb_recv.at[CHUNKS])
     lax.fori_loop(2, 4, middle_step, 0)
     lax.fori_loop(0, CHUNKS, send_upper, 0)
     recv_b[:, pl.ds(16 * n, 16)] = half_b[:, n]

time: 94.2 us -> 90.8 us (0.964)
  Pallas kernels: 92.7 us -> 89.4 us
    pallas_call x1, Pallas kernels: 92.7 us -> 89.4 us  [on_device(): pl.pallas_call(kernel, out_shape=pltpu.VMEM((8, 64, 1024), F32), in_specs...]
where the time goes in v4:
time: 90.8 us; the launch traced here: 90.7 us
  Pallas kernels  89.4 us (98%)
  local copies, waits for them, and re-layouts  1.32 us (1%)
    pallas_call x1, Pallas kernels, on_device(): pl.pallas_call(kernel, out_shape=pltpu.VMEM((8, 64, 1024), F32), in_specs...  89.4 us

profile of v4, /device:TPU:1, one launch (start us, length us, event | category | flops | bytes accessed | tf_op | source)
XLA Modules:
  0.0 90.7 jit_solution(18348565157019299172)
XLA Ops:
  0.0 89.4 %shard_map.82 = f32[8,64,1024]{2,1,0:T(8,128)S(1)} custom-call(f32[512,16,512]{2,1,0:T(8,128)} %source.1, bf16[2,256,512]{2,1,0:T(8,128)(2,1)} %constant.8.clone.x_hbm, bf16[2,256,512]{2,1,0:T(8,128)(2,1)} %constant.9.clone.y_hbm, f32[2,128,1024]{2,1,0:T(8,128)} %constant.10.clone.fine_hbm, f32[2,16,1024]{2,1,0:T(8,128)} %constant.11.clone.coarse_hbm, ...), custom_call_target="tpu_custom_call" | custom-call | tf_op jit(solution)/shard_map/pallas_call | solution.py:354
  89.4 1.3 %copy.10 = f32[8,64,1024]{2,1,0:T(8,128)} copy(f32[8,64,1024]{2,1,0:T(8,128)S(1)} %shard_map.82) | data formatting | bytes 4194304

commit v5 on v4

--- a/solution.py
+++ b/solution.py
@@ -203,12 +203,13 @@
             jnp.sum(picked, axis=1, keepdims=True), (128, 128)
         )
 
-    def z_stage(load_block, rows, store):
+    def z_left(load_block, rows):
         for b in range(16):
             high, low = split(load_block(b))
             left_high[0:rows, b * 128 : b * 128 + 128] = high
             left_low[0:rows, b * 128 : b * 128 + 128] = low
 
+    def z_cols(rows, store, start, stop):
         def col_step(t, _):
             cols = pl.ds(pl.multiple_of(t * 256, 256), 256)
             res = dot3(
@@ -217,7 +218,7 @@
             store(t, cols, res)
             return 0
 
-        lax.fori_loop(0, 4, col_step, 0)
+        lax.fori_loop(start, stop, col_step, 0)
 
     def step_a(s):
         wait_bytes(gath_a.at[s, :, pl.ds(0, 496)], na_recv.at[s])
@@ -253,7 +254,8 @@
                             at : at + 8, c * 128 : c * 128 + 128
                         ]
 
-        z_stage(lambda b: gath_b[q, b // 4, b % 4].reshape(128, 128), 128, store)
+        z_left(lambda b: gath_b[q, b // 4, b % 4].reshape(128, 128), 128)
+        z_cols(128, store, 0, 4)
 
     def send_half_b(modes, half, sem):
         for offset in peer_order():
@@ -279,8 +281,10 @@
 
     lax.fori_loop(0, 2, lambda q, c: (step_b(q), c)[1], 0)
     send_half_b(pl.ds(0, 8), 0, nb_recv.at[CHUNKS])
-    lax.fori_loop(2, 4, middle_step, 0)
+    lax.fori_loop(2, 3, middle_step, 0)
+    step_b(3)
     lax.fori_loop(0, CHUNKS, send_upper, 0)
+    lax.fori_loop(2, 4, lambda s, c: (step_a(s), c)[1], 0)
     recv_b[:, pl.ds(16 * n, 16)] = half_b[:, n]
     wait_bytes(recv_b.at[:, pl.ds(0, 248)], nb_recv.at[CHUNKS])
 
@@ -304,16 +308,17 @@
         out[4 + d, :, cols] = last_b[pl.ds(64 * d, 64), cols]
         return 0
 
-    lax.fori_loop(0, CHUNKS, last_step, 0)
-
-    wait_bytes(recv_a.at[pl.ds(0, 3)], y2_recv)
-
     def store_a(t, cols, res):
         for i in range(4):
             symbol = (sym_x[8 * n + i] + col_y[pl.ds(64 * d, 64), 0:1]) + sym_z[0:1, cols]
             out[i, :, cols] = res[i * 64 : i * 64 + 64] * lax.rsqrt(symbol)
 
-    z_stage(lambda b: recv_a[b // 4, b % 4].reshape(256, 128), 256, store_a)
+    lax.fori_loop(0, 5, last_step, 0)
+    wait_bytes(recv_a.at[pl.ds(0, 3)], y2_recv)
+    z_left(lambda b: recv_a[b // 4, b % 4].reshape(256, 128), 256)
+    z_cols(256, store_a, 0, 2)
+    lax.fori_loop(5, CHUNKS, last_step, 0)
+    z_cols(256, store_a, 2, 4)
 
     wait_bytes(first_a.at[:, pl.ds(0, 124)], na_send)
     wait_bytes(gath_b.at[:, pl.ds(0, 3)], y1_send)

time: 90.8 us -> 92.3 us (1.017)
  Pallas kernels: 89.4 us -> 90.8 us
    pallas_call x1, Pallas kernels: 89.4 us -> 90.8 us  [on_device(): pl.pallas_call(kernel, out_shape=pltpu.VMEM((8, 64, 1024), F32), in_specs...]
where the time goes in v5:
time: 92.3 us; the launch traced here: 92.2 us
  Pallas kernels  90.8 us (98%)
  local copies, waits for them, and re-layouts  1.32 us (1%)
    pallas_call x1, Pallas kernels, on_device(): pl.pallas_call(kernel, out_shape=pltpu.VMEM((8, 64, 1024), F32), in_specs...  90.8 us

profile of v5, /device:TPU:1, one launch (start us, length us, event | category | flops | bytes accessed | tf_op | source)
XLA Modules:
  0.0 92.2 jit_solution(12899205720629631965)
XLA Ops:
  0.0 90.8 %shard_map.82 = f32[8,64,1024]{2,1,0:T(8,128)S(1)} custom-call(f32[512,16,512]{2,1,0:T(8,128)} %source.1, bf16[2,256,512]{2,1,0:T(8,128)(2,1)} %constant.8.clone.x_hbm, bf16[2,256,512]{2,1,0:T(8,128)(2,1)} %constant.9.clone.y_hbm, f32[2,128,1024]{2,1,0:T(8,128)} %constant.10.clone.fine_hbm, f32[2,16,1024]{2,1,0:T(8,128)} %constant.11.clone.coarse_hbm, ...), custom_call_target="tpu_custom_call" | custom-call | tf_op jit(solution)/shard_map/pallas_call | solution.py:359
  90.9 1.3 %copy.10 = f32[8,64,1024]{2,1,0:T(8,128)} copy(f32[8,64,1024]{2,1,0:T(8,128)S(1)} %shard_map.82) | data formatting | bytes 4194304
